TPU v7x, 1024 devices: a whole 4x8x16 slice. The times are simulated.
1024 devices in a mesh: gx: 8 (over z_lo), gy: 4 (over z_hi, core), ta: 32 (over x, y).
Axes of the slice: x: 4, y: 8, z: 16 (z_hi: 2, z_lo: 8; z = z_hi * 8 + z_lo), core: 2. Of those that a mesh axis runs over, the one named last changes fastest.
Arguments:
- links: float32 [4, 2, 3, 3, 16, 8, 32, 128], P(None, None, None, None, 'gx', 'gy', 'ta'), may hold values from -1 to 1, as said below
Outputs:
- flowed: float32 [4, 2, 3, 3, 16, 8, 32, 128], P(None, None, None, None, 'gx', 'gy', 'ta')
- action_slices: float32 [32], P('ta')
Inputs may be any that keep to these rules, and one draw needn't show every extreme that they name: `links`: every link is a special unitary 3x3 matrix.
All inputs are finite; a program needn't handle non-finite values.
Results may differ from a plain program's by a relative error of at most 0.0003.
Values sent between devices are 32-bit elements; how exact they have to be, the bound alone decides.
No kernel may reach another device: no remote copies, remote signals or barrier semaphores. Data moves between devices by JAX's collectives and lax.ppermute only.
A program may use at most 32 MiB of HBM per device.

v0:
```python
import jax
import jax.numpy as jnp
from jax import lax
from jax.sharding import PartitionSpec as P

flow_eps = 0.1
taylor_order = 6


def padded_2(shard, sides, width):
    for axis, dim in sides:
        devices, length = (lax.axis_size(axis), shard.shape[dim])
        up = [(i, (i + 1) % devices) for i in range(devices)]
        down = [(j, i) for i, j in up]
        last = lax.slice_in_dim(shard, length - width, length, axis=dim)
        initial = lax.slice_in_dim(shard, 0, width, axis=dim)
        before = lax.ppermute(last, axis, up)
        after = lax.ppermute(initial, axis, down)
        shard = jnp.concatenate([before, shard, after], axis=dim)
    return shard


def sent_to_all(shard, axis):
    devices = lax.axis_size(axis)
    return lax.all_to_all(
        jnp.broadcast_to(shard[None], (devices, *shard.shape)), axis, 0, 0, tiled=True
    )


def taken_together(shard, axis):
    everything = sent_to_all(shard, axis)
    return jnp.sum(everything, axis=0)


def contract(first_part, second_part):
    return jnp.sum(first_part[:, :, None] * second_part[None, :, :], axis=1)


def matmul_pair(former, latter):
    return jnp.stack(
        [
            contract(former[0], latter[0]) - contract(former[1], latter[1]),
            contract(former[0], latter[1]) + contract(former[1], latter[0]),
        ]
    )


def adjoint(matrix):
    return jnp.stack([jnp.swapaxes(matrix[0], 0, 1), -jnp.swapaxes(matrix[1], 0, 1)])


def trace_real(former, latter):
    return jnp.sum(
        former[0] * jnp.swapaxes(latter[0], 0, 1) - former[1] * jnp.swapaxes(latter[1], 0, 1),
        axis=(0, 1),
    )


def unit_offset(dir_index, sign):
    return tuple((sign if k == dir_index else 0 for k in range(4)))


def add_offsets(first_off, second_off):
    return tuple((first_off[k] + second_off[k] for k in range(4)))


def shifted(component, offset):
    x_len = component.shape[-4] - 2
    y_len = component.shape[-3] - 2
    t_len = component.shape[-2] - 2
    view = component[
        ...,
        1 + offset[0] : 1 + offset[0] + x_len,
        1 + offset[1] : 1 + offset[1] + y_len,
        1 + offset[2] : 1 + offset[2] + t_len,
        :,
    ]
    if offset[3] != 0:
        view = jnp.roll(view, -offset[3], axis=-1)
    return view


def upper_staple(padded, mu_dir, nu_dir):
    here = (0, 0, 0, 0)
    first_pair = matmul_pair(
        shifted(padded[nu_dir], unit_offset(mu_dir, 1)),
        adjoint(shifted(padded[mu_dir], unit_offset(nu_dir, 1))),
    )
    return matmul_pair(first_pair, adjoint(shifted(padded[nu_dir], here)))


def lower_corner(padded, mu_dir, nu_dir):
    back = unit_offset(nu_dir, -1)
    corner = add_offsets(unit_offset(mu_dir, 1), back)
    first_pair = matmul_pair(
        adjoint(shifted(padded[nu_dir], corner)), adjoint(shifted(padded[mu_dir], back))
    )
    return matmul_pair(first_pair, shifted(padded[nu_dir], back))


def antihermitian(matrix):
    real_part = (matrix[0] - jnp.swapaxes(matrix[0], 0, 1)) / 2.0
    imag_part = (matrix[1] + jnp.swapaxes(matrix[1], 0, 1)) / 2.0
    trace_imag = jnp.trace(matrix[1], axis1=0, axis2=1) / 3.0
    eye = jnp.eye(3, dtype=jnp.float32).reshape((3, 3) + (1,) * (matrix.ndim - 3))
    return jnp.stack([real_part, imag_part - eye * trace_imag])


def flow_force(padded, lower_fn):
    centre = padded[..., 1:-1, 1:-1, 1:-1, :]
    forces = []
    action = jnp.zeros((centre.shape[6],), jnp.float32)
    for mu_dir in range(4):
        link_here = centre[mu_dir]
        staple_sum = jnp.zeros_like(link_here)
        for nu_dir in range(4):
            if nu_dir == mu_dir:
                continue
            upper = upper_staple(padded, mu_dir, nu_dir)
            action = action + jnp.sum(1.0 - trace_real(link_here, upper) / 3.0, axis=(0, 1, 3))
            staple_sum = staple_sum + upper + lower_fn(mu_dir, nu_dir)
        omega = matmul_pair(link_here, staple_sum)
        forces.append(-flow_eps * antihermitian(omega))
    return (jnp.stack(forces), action / 2.0)


def polynomial_exp(generator):
    eye = jnp.eye(3, dtype=jnp.float32).reshape((3, 3) + (1,) * (generator.ndim - 3))
    identity = jnp.stack(
        [jnp.broadcast_to(eye, generator.shape[1:]), jnp.zeros(generator.shape[1:], jnp.float32)]
    )
    result = identity
    for order in range(taylor_order, 0, -1):
        result = identity + matmul_pair(generator, result) / order
    return result


def advance(generator, links_now):

    def one_direction(gen_dir, link_dir):
        return matmul_pair(polynomial_exp(gen_dir), link_dir)

    return jax.vmap(one_direction)(generator, links_now)


def section_force(links_now):
    padded = padded_2(links_now, (("gx", 4), ("gy", 5), ("ta", 6)), 1)

    def lower_fn(mu_dir, nu_dir):
        return lower_corner(padded, mu_dir, nu_dir)

    return flow_force(padded, lower_fn)


def local(links):
    force_zero, action = section_force(links)
    section_one = advance(force_zero / 4.0, links)
    force_one, unused_one = section_force(section_one)
    section_two = advance(8.0 / 9.0 * force_one - 17.0 / 36.0 * force_zero, section_one)
    force_two, unused_two = section_force(section_two)
    flowed = advance(
        3.0 / 4.0 * force_two - 8.0 / 9.0 * force_one + 17.0 / 36.0 * force_zero, section_two
    )
    total = taken_together(action, ("gx", "gy"))
    sites_slice = (
        6.0
        * links.shape[4]
        * lax.axis_size("gx")
        * links.shape[5]
        * lax.axis_size("gy")
        * links.shape[7]
    )
    return (flowed, total / sites_slice)


def solution(mesh):
    placed = (P(None, None, None, None, "gx", "gy", "ta", None),)
    return jax.shard_map(
        local,
        mesh=mesh,
        in_specs=placed,
        out_specs=(P(None, None, None, None, "gx", "gy", "ta", None), P("ta")),
        check_vma=False,
    )
```

profile of v0, /device:TPU:1, one launch (start us, length us, event | category | flops | bytes accessed | tf_op | source)
XLA Modules:
  0.0 273.0 jit_solution(16230578829092830676)
XLA Ops:
  0.6 1.0 fusion.394
  1.7 4.8 %collective-permute-start = (f32[4,2,3,3,1,2,1,128]{7,6,5,4,3,2,1,0:T(1,128)S(1)}, f32[4,2,3,3,1,2,1,128]{7,6,5,4,3,2,1,0:T(1,128)S(1)}, u32[]{:S(2)}, u32[]{:S(2)}) collective-permute-start(f32[4,2,3,3,1,2,1,128]{7,6,5,4,3,2,1,0:T(1,128)S(1)} %get-tuple-element.1161), channel_id=1, source_target_pairs={{0,128},{128,256},{256,384},{384,512},{512,640},{640,768},{768,896... | collective-permute-start | bytes 221192 | tf_op jit(solution)/shard_map/ppermute | solution.py:17
  6.5 14.0 %collective-permute-start.1 = (f32[4,2,3,3,1,2,1,128]{7,6,5,4,3,2,1,0:T(1,128)S(1)}, f32[4,2,3,3,1,2,1,128]{7,6,5,4,3,2,1,0:T(1,128)S(1)}, u32[]{:S(2)}, u32[]{:S(2)}) collective-permute-start(f32[4,2,3,3,1,2,1,128]{7,6,5,4,3,2,1,0:T(1,128)S(1)} %get-tuple-element.1160), channel_id=1, source_target_pairs={{128,0},{256,128},{384,256},{512,384},{640,512},{768,640},{896,768... | collective-permute-start | bytes 221192 | tf_op jit(solution)/shard_map/ppermute | solution.py:18
  20.5 1.0 constant_dynamic-update-slice_fusion.1
  22.1 14.7 %collective-permute-start.2 = (f32[4,2,3,3,4,1,1,128]{7,6,5,4,3,2,1,0:T(1,128)S(1)}, f32[4,2,3,3,4,1,1,128]{7,6,5,4,3,2,1,0:T(1,128)S(1)}, u32[]{:S(2)}, u32[]{:S(2)}) collective-permute-start(f32[4,2,3,3,4,1,1,128]{7,6,5,4,3,2,1,0:T(1,128)S(1)} %get-tuple-element.1081), channel_id=1, source_target_pairs={{0,32},{32,64},{64,96},{96,0},{1,33},{33,65},{65,97},{97,1},{2,34}... | collective-permute-start | bytes 442376 | tf_op jit(solution)/shard_map/ppermute | solution.py:17
  36.8 1.9 collective-permute-start.3
  38.7 0.8 collective-permute-done.2
  39.5 15.6 %collective-permute-done.3 = f32[4,2,3,3,4,1,1,128]{7,6,5,4,3,2,1,0:T(1,128)S(1)} collective-permute-done((f32[4,2,3,3,4,1,1,128]{7,6,5,4,3,2,1,0:T(1,128)S(1)}, f32[4,2,3,3,4,1,1,128]{7,6,5,4,3,2,1,0:T(1,128)S(1)}, u32[]{:S(2)}, u32[]{:S(2)}) %collective-permute-start.3) | collective-permute-done | bytes 147488 | tf_op jit(solution)/shard_map/ppermute | solution.py:18
  55.7 2.6 collective-permute-start.4
  58.3 6.0 %collective-permute-start.5 = (f32[4,2,3,3,4,4,1,128]{7,6,5,4,3,2,1,0:T(1,128)S(1)}, f32[4,2,3,3,4,4,1,128]{7,6,5,4,3,2,1,0:T(1,128)S(1)}, u32[]{:S(2)}, u32[]{:S(2)}) collective-permute-start(f32[4,2,3,3,4,4,1,128]{7,6,5,4,3,2,1,0:T(1,128)S(1)} %pad_maximum_fusion.3), channel_id=1, source_target_pairs={{1,0},{2,1},{3,2},{4,3},{5,4},{6,5},{7,6},{8,7},{9,8},{10,9},{11,1... | collective-permute-start | bytes 1769480 | tf_op jit(solution)/shard_map/ppermute | solution.py:18
  64.9 6.5 %collective-permute-done.4 = f32[4,2,3,3,4,4,1,128]{7,6,5,4,3,2,1,0:T(1,128)S(1)} collective-permute-done((f32[4,2,3,3,4,4,1,128]{7,6,5,4,3,2,1,0:T(1,128)S(1)}, f32[4,2,3,3,4,4,1,128]{7,6,5,4,3,2,1,0:T(1,128)S(1)}, u32[]{:S(2)}, u32[]{:S(2)}) %collective-permute-start.4) | collective-permute-done | bytes 589856 | tf_op jit(solution)/shard_map/ppermute | solution.py:17
  71.4 1.8 collective-permute-done.5
  73.1 2.0 pad_maximum_fusion
  75.1 0.8 slice_bitcast_fusion
  87.9 0.7 fusion.62
  91.0 0.7 subtract_reduce_fusion.2
  92.2 0.6 subtract_reduce_fusion.8
  95.5 1.9 collective-permute-start.6
  97.4 10.0 %collective-permute-start.7 = (f32[4,2,3,3,1,2,1,128]{7,0,5,4,3,2,6,1:T(4,128)S(1)}, f32[4,2,3,3,1,2,1,128]{7,0,5,4,3,2,6,1:T(4,128)S(1)}, u32[]{:S(2)}, u32[]{:S(2)}) collective-permute-start(f32[4,2,3,3,1,2,1,128]{7,0,5,4,3,2,6,1:T(4,128)S(1)} %get-tuple-element.1135), channel_id=1, source_target_pairs={{128,0},{256,128},{384,256},{512,384},{640,512},{768,640},{896,768... | collective-permute-start | bytes 221192 | tf_op jit(solution)/shard_map/ppermute | solution.py:18
  107.4 0.6 subtract_reduce_fusion.10
  108.0 1.6 collective-permute-done.7
  109.7 9.0 %collective-permute-start.8 = (f32[4,2,3,3,4,1,1,128]{7,0,5,4,3,2,6,1:T(4,128)S(1)}, f32[4,2,3,3,4,1,1,128]{7,0,5,4,3,2,6,1:T(4,128)S(1)}, u32[]{:S(2)}, u32[]{:S(2)}) collective-permute-start(f32[4,2,3,3,4,1,1,128]{7,0,5,4,3,2,6,1:T(4,128)S(1)} %get-tuple-element.1079), channel_id=1, source_target_pairs={{0,32},{32,64},{64,96},{96,0},{1,33},{33,65},{65,97},{97,1},{2,34}... | collective-permute-start | bytes 442376 | tf_op jit(solution)/shard_map/ppermute | solution.py:17
  118.7 1.9 collective-permute-start.9
  120.7 0.6 subtract_reduce_fusion.11
  121.3 0.7 subtract_reduce_fusion.9
  121.9 12.0 %collective-permute-done.9 = f32[4,2,3,3,4,1,1,128]{7,0,5,4,3,2,6,1:T(4,128)S(1)} collective-permute-done((f32[4,2,3,3,4,1,1,128]{7,0,5,4,3,2,6,1:T(4,128)S(1)}, f32[4,2,3,3,4,1,1,128]{7,0,5,4,3,2,6,1:T(4,128)S(1)}, u32[]{:S(2)}, u32[]{:S(2)}) %collective-permute-start.9) | collective-permute-done | bytes 147488 | tf_op jit(solution)/shard_map/ppermute | solution.py:18
  134.1 1.9 collective-permute-start.10
  136.0 7.1 %collective-permute-start.11 = (f32[4,2,3,3,4,4,1,128]{7,0,5,4,3,2,6,1:T(4,128)S(1)}, f32[4,2,3,3,4,4,1,128]{7,0,5,4,3,2,6,1:T(4,128)S(1)}, u32[]{:S(2)}, u32[]{:S(2)}) collective-permute-start(f32[4,2,3,3,4,4,1,128]{7,0,5,4,3,2,6,1:T(4,128)S(1)} %pad_maximum_fusion.4), channel_id=1, source_target_pairs={{1,0},{2,1},{3,2},{4,3},{5,4},{6,5},{7,6},{8,7},{9,8},{10,9},{11,1... | collective-permute-start | bytes 1769480 | tf_op jit(solution)/shard_map/ppermute | solution.py:18
  143.1 0.7 subtract_reduce_fusion.7
  144.5 3.9 %collective-permute-done.10 = f32[4,2,3,3,4,4,1,128]{7,0,5,4,3,2,6,1:T(4,128)S(1)} collective-permute-done((f32[4,2,3,3,4,4,1,128]{7,0,5,4,3,2,6,1:T(4,128)S(1)}, f32[4,2,3,3,4,4,1,128]{7,0,5,4,3,2,6,1:T(4,128)S(1)}, u32[]{:S(2)}, u32[]{:S(2)}) %collective-permute-start.10) | collective-permute-done | bytes 589856 | tf_op jit(solution)/shard_map/ppermute | solution.py:17
  148.5 1.5 collective-permute-done.11
  150.4 1.3 fusion.359
  167.4 1.9 collective-permute-start.12
  169.4 10.8 %collective-permute-start.13 = (f32[4,2,3,3,1,2,1,128]{7,0,5,4,3,2,6,1:T(4,128)S(1)}, f32[4,2,3,3,1,2,1,128]{7,0,5,4,3,2,6,1:T(4,128)S(1)}, u32[]{:S(2)}, u32[]{:S(2)}) collective-permute-start(f32[4,2,3,3,1,2,1,128]{7,0,5,4,3,2,6,1:T(4,128)S(1)} %get-tuple-element.1109), channel_id=1, source_target_pairs={{128,0},{256,128},{384,256},{512,384},{640,512},{768,640},{896,768... | collective-permute-start | bytes 221192 | tf_op jit(solution)/shard_map/ppermute | solution.py:18
  180.2 0.6 subtract_reduce_fusion.4
  180.8 0.8 collective-permute-done.13
  181.7 12.4 %collective-permute-start.14 = (f32[4,2,3,3,4,1,1,128]{7,0,5,4,3,2,6,1:T(4,128)S(1)}, f32[4,2,3,3,4,1,1,128]{7,0,5,4,3,2,6,1:T(4,128)S(1)}, u32[]{:S(2)}, u32[]{:S(2)}) collective-permute-start(f32[4,2,3,3,4,1,1,128]{7,0,5,4,3,2,6,1:T(4,128)S(1)} %get-tuple-element.1077), channel_id=1, source_target_pairs={{0,32},{32,64},{64,96},{96,0},{1,33},{33,65},{65,97},{97,1},{2,34}... | collective-permute-start | bytes 442376 | tf_op jit(solution)/shard_map/ppermute | solution.py:17
  194.1 1.9 collective-permute-start.15
  196.0 0.6 subtract_reduce_fusion.3
  196.6 0.6 subtract_reduce_fusion.1
  197.7 11.6 %collective-permute-done.15 = f32[4,2,3,3,4,1,1,128]{7,0,5,4,3,2,6,1:T(4,128)S(1)} collective-permute-done((f32[4,2,3,3,4,1,1,128]{7,0,5,4,3,2,6,1:T(4,128)S(1)}, f32[4,2,3,3,4,1,1,128]{7,0,5,4,3,2,6,1:T(4,128)S(1)}, u32[]{:S(2)}, u32[]{:S(2)}) %collective-permute-start.15) | collective-permute-done | bytes 147488 | tf_op jit(solution)/shard_map/ppermute | solution.py:18
  209.4 1.9 collective-permute-start.16
  211.4 9.6 %collective-permute-start.17 = (f32[4,2,3,3,4,4,1,128]{7,0,5,4,3,2,6,1:T(4,128)S(1)}, f32[4,2,3,3,4,4,1,128]{7,0,5,4,3,2,6,1:T(4,128)S(1)}, u32[]{:S(2)}, u32[]{:S(2)}) collective-permute-start(f32[4,2,3,3,4,4,1,128]{7,0,5,4,3,2,6,1:T(4,128)S(1)} %pad_maximum_fusion.5), channel_id=1, source_target_pairs={{1,0},{2,1},{3,2},{4,3},{5,4},{6,5},{7,6},{8,7},{9,8},{10,9},{11,1... | collective-permute-start | bytes 1769480 | tf_op jit(solution)/shard_map/ppermute | solution.py:18
  221.0 0.7 subtract_reduce_fusion
  229.2 22.6 %all_to_all.6 = f32[32,1,1]{2,1,0:T(1,128)S(1)} all-to-all(f32[32,1,1]{2,1,0:T(1,128)S(1)} %broadcast_in_dim.106), channel_id=1, replica_groups=mesh['gx'=8,'gy'=4,'ta'=32] {'gx','gy'}, dimensions={0} | all-to-all | bytes 256 | tf_op jit(solution)/shard_map/all_to_all | solution.py:25
  251.7 0.6 reduce_sum.7474
  253.7 1.3 fusion.358
  270.8 0.8 copy.1458
  (702 shorter events, 49.5 us)
Async XLA Ops:
  0.6 63.9 %copy-start = (f32[4,2,3,3,2,2,1,128]{7,6,5,4,3,2,1,0:T(1,128)S(1)}, f32[4,2,3,3,2,2,1,128]{7,6,5,4,3,2,1,0:T(1,128)}, u32[]{:S(2)}) copy-start(f32[4,2,3,3,2,2,1,128]{7,6,5,4,3,2,1,0:T(1,128)} %param.1) | copy-start | bytes 442372
  1.7 18.8 %collective-permute-start = (f32[4,2,3,3,1,2,1,128]{7,6,5,4,3,2,1,0:T(1,128)S(1)}, f32[4,2,3,3,1,2,1,128]{7,6,5,4,3,2,1,0:T(1,128)S(1)}, u32[]{:S(2)}, u32[]{:S(2)}) collective-permute-start(f32[4,2,3,3,1,2,1,128]{7,6,5,4,3,2,1,0:T(1,128)S(1)} %get-tuple-element.1161), channel_id=1, source_target_pairs={{0,128},{128,256},{256,384},{384,512},{512,640},{640,768},{768,896... | collective-permute-start | bytes 221192 | tf_op jit(solution)/shard_map/ppermute | solution.py:17
  6.5 15.4 %collective-permute-start.1 = (f32[4,2,3,3,1,2,1,128]{7,6,5,4,3,2,1,0:T(1,128)S(1)}, f32[4,2,3,3,1,2,1,128]{7,6,5,4,3,2,1,0:T(1,128)S(1)}, u32[]{:S(2)}, u32[]{:S(2)}) collective-permute-start(f32[4,2,3,3,1,2,1,128]{7,6,5,4,3,2,1,0:T(1,128)S(1)} %get-tuple-element.1160), channel_id=1, source_target_pairs={{128,0},{256,128},{384,256},{512,384},{640,512},{768,640},{896,768... | collective-permute-start | bytes 221192 | tf_op jit(solution)/shard_map/ppermute | solution.py:18
  22.1 17.4 %collective-permute-start.2 = (f32[4,2,3,3,4,1,1,128]{7,6,5,4,3,2,1,0:T(1,128)S(1)}, f32[4,2,3,3,4,1,1,128]{7,6,5,4,3,2,1,0:T(1,128)S(1)}, u32[]{:S(2)}, u32[]{:S(2)}) collective-permute-start(f32[4,2,3,3,4,1,1,128]{7,6,5,4,3,2,1,0:T(1,128)S(1)} %get-tuple-element.1081), channel_id=1, source_target_pairs={{0,32},{32,64},{64,96},{96,0},{1,33},{33,65},{65,97},{97,1},{2,34}... | collective-permute-start | bytes 442376 | tf_op jit(solution)/shard_map/ppermute | solution.py:17
  36.8 18.4 %collective-permute-start.3 = (f32[4,2,3,3,4,1,1,128]{7,6,5,4,3,2,1,0:T(1,128)S(1)}, f32[4,2,3,3,4,1,1,128]{7,6,5,4,3,2,1,0:T(1,128)S(1)}, u32[]{:S(2)}, u32[]{:S(2)}) collective-permute-start(f32[4,2,3,3,4,1,1,128]{7,6,5,4,3,2,1,0:T(1,128)S(1)} %get-tuple-element.1082), channel_id=1, source_target_pairs={{32,0},{64,32},{96,64},{0,96},{33,1},{65,33},{97,65},{1,97},{34,2}... | collective-permute-start | bytes 442376 | tf_op jit(solution)/shard_map/ppermute | solution.py:18
  55.7 15.6 %collective-permute-start.4 = (f32[4,2,3,3,4,4,1,128]{7,6,5,4,3,2,1,0:T(1,128)S(1)}, f32[4,2,3,3,4,4,1,128]{7,6,5,4,3,2,1,0:T(1,128)S(1)}, u32[]{:S(2)}, u32[]{:S(2)}) collective-permute-start(f32[4,2,3,3,4,4,1,128]{7,6,5,4,3,2,1,0:T(1,128)S(1)} %pad_maximum_fusion.3), channel_id=1, source_target_pairs={{0,1},{1,2},{2,3},{3,4},{4,5},{5,6},{6,7},{7,8},{8,9},{9,10},{10,1... | collective-permute-start | bytes 1769480 | tf_op jit(solution)/shard_map/ppermute | solution.py:17
  58.3 14.8 %collective-permute-start.5 = (f32[4,2,3,3,4,4,1,128]{7,6,5,4,3,2,1,0:T(1,128)S(1)}, f32[4,2,3,3,4,4,1,128]{7,6,5,4,3,2,1,0:T(1,128)S(1)}, u32[]{:S(2)}, u32[]{:S(2)}) collective-permute-start(f32[4,2,3,3,4,4,1,128]{7,6,5,4,3,2,1,0:T(1,128)S(1)} %pad_maximum_fusion.3), channel_id=1, source_target_pairs={{1,0},{2,1},{3,2},{4,3},{5,4},{6,5},{7,6},{8,7},{9,8},{10,9},{11,1... | collective-permute-start | bytes 1769480 | tf_op jit(solution)/shard_map/ppermute | solution.py:18
  95.5 12.5 %collective-permute-start.6 = (f32[4,2,3,3,1,2,1,128]{7,0,5,4,3,2,6,1:T(4,128)S(1)}, f32[4,2,3,3,1,2,1,128]{7,0,5,4,3,2,6,1:T(4,128)S(1)}, u32[]{:S(2)}, u32[]{:S(2)}) collective-permute-start(f32[4,2,3,3,1,2,1,128]{7,0,5,4,3,2,6,1:T(4,128)S(1)} %get-tuple-element.1134), channel_id=1, source_target_pairs={{0,128},{128,256},{256,384},{384,512},{512,640},{640,768},{768,896... | collective-permute-start | bytes 221192 | tf_op jit(solution)/shard_map/ppermute | solution.py:17
  97.4 12.2 %collective-permute-start.7 = (f32[4,2,3,3,1,2,1,128]{7,0,5,4,3,2,6,1:T(4,128)S(1)}, f32[4,2,3,3,1,2,1,128]{7,0,5,4,3,2,6,1:T(4,128)S(1)}, u32[]{:S(2)}, u32[]{:S(2)}) collective-permute-start(f32[4,2,3,3,1,2,1,128]{7,0,5,4,3,2,6,1:T(4,128)S(1)} %get-tuple-element.1135), channel_id=1, source_target_pairs={{128,0},{256,128},{384,256},{512,384},{640,512},{768,640},{896,768... | collective-permute-start | bytes 221192 | tf_op jit(solution)/shard_map/ppermute | solution.py:18
  109.7 12.2 %collective-permute-start.8 = (f32[4,2,3,3,4,1,1,128]{7,0,5,4,3,2,6,1:T(4,128)S(1)}, f32[4,2,3,3,4,1,1,128]{7,0,5,4,3,2,6,1:T(4,128)S(1)}, u32[]{:S(2)}, u32[]{:S(2)}) collective-permute-start(f32[4,2,3,3,4,1,1,128]{7,0,5,4,3,2,6,1:T(4,128)S(1)} %get-tuple-element.1079), channel_id=1, source_target_pairs={{0,32},{32,64},{64,96},{96,0},{1,33},{33,65},{65,97},{97,1},{2,34}... | collective-permute-start | bytes 442376 | tf_op jit(solution)/shard_map/ppermute | solution.py:17
  118.7 15.2 %collective-permute-start.9 = (f32[4,2,3,3,4,1,1,128]{7,0,5,4,3,2,6,1:T(4,128)S(1)}, f32[4,2,3,3,4,1,1,128]{7,0,5,4,3,2,6,1:T(4,128)S(1)}, u32[]{:S(2)}, u32[]{:S(2)}) collective-permute-start(f32[4,2,3,3,4,1,1,128]{7,0,5,4,3,2,6,1:T(4,128)S(1)} %get-tuple-element.1080), channel_id=1, source_target_pairs={{32,0},{64,32},{96,64},{0,96},{33,1},{65,33},{97,65},{1,97},{34,2}... | collective-permute-start | bytes 442376 | tf_op jit(solution)/shard_map/ppermute | solution.py:18
  134.1 14.4 %collective-permute-start.10 = (f32[4,2,3,3,4,4,1,128]{7,0,5,4,3,2,6,1:T(4,128)S(1)}, f32[4,2,3,3,4,4,1,128]{7,0,5,4,3,2,6,1:T(4,128)S(1)}, u32[]{:S(2)}, u32[]{:S(2)}) collective-permute-start(f32[4,2,3,3,4,4,1,128]{7,0,5,4,3,2,6,1:T(4,128)S(1)} %pad_maximum_fusion.4), channel_id=1, source_target_pairs={{0,1},{1,2},{2,3},{3,4},{4,5},{5,6},{6,7},{7,8},{8,9},{9,10},{10,1... | collective-permute-start | bytes 1769480 | tf_op jit(solution)/shard_map/ppermute | solution.py:17
  136.0 13.9 %collective-permute-start.11 = (f32[4,2,3,3,4,4,1,128]{7,0,5,4,3,2,6,1:T(4,128)S(1)}, f32[4,2,3,3,4,4,1,128]{7,0,5,4,3,2,6,1:T(4,128)S(1)}, u32[]{:S(2)}, u32[]{:S(2)}) collective-permute-start(f32[4,2,3,3,4,4,1,128]{7,0,5,4,3,2,6,1:T(4,128)S(1)} %pad_maximum_fusion.4), channel_id=1, source_target_pairs={{1,0},{2,1},{3,2},{4,3},{5,4},{6,5},{7,6},{8,7},{9,8},{10,9},{11,1... | collective-permute-start | bytes 1769480 | tf_op jit(solution)/shard_map/ppermute | solution.py:18
  167.4 13.4 %collective-permute-start.12 = (f32[4,2,3,3,1,2,1,128]{7,0,5,4,3,2,6,1:T(4,128)S(1)}, f32[4,2,3,3,1,2,1,128]{7,0,5,4,3,2,6,1:T(4,128)S(1)}, u32[]{:S(2)}, u32[]{:S(2)}) collective-permute-start(f32[4,2,3,3,1,2,1,128]{7,0,5,4,3,2,6,1:T(4,128)S(1)} %get-tuple-element.1108), channel_id=1, source_target_pairs={{0,128},{128,256},{256,384},{384,512},{512,640},{640,768},{768,896... | collective-permute-start | bytes 221192 | tf_op jit(solution)/shard_map/ppermute | solution.py:17
  169.4 12.2 %collective-permute-start.13 = (f32[4,2,3,3,1,2,1,128]{7,0,5,4,3,2,6,1:T(4,128)S(1)}, f32[4,2,3,3,1,2,1,128]{7,0,5,4,3,2,6,1:T(4,128)S(1)}, u32[]{:S(2)}, u32[]{:S(2)}) collective-permute-start(f32[4,2,3,3,1,2,1,128]{7,0,5,4,3,2,6,1:T(4,128)S(1)} %get-tuple-element.1109), channel_id=1, source_target_pairs={{128,0},{256,128},{384,256},{512,384},{640,512},{768,640},{896,768... | collective-permute-start | bytes 221192 | tf_op jit(solution)/shard_map/ppermute | solution.py:18
  181.7 16.0 %collective-permute-start.14 = (f32[4,2,3,3,4,1,1,128]{7,0,5,4,3,2,6,1:T(4,128)S(1)}, f32[4,2,3,3,4,1,1,128]{7,0,5,4,3,2,6,1:T(4,128)S(1)}, u32[]{:S(2)}, u32[]{:S(2)}) collective-permute-start(f32[4,2,3,3,4,1,1,128]{7,0,5,4,3,2,6,1:T(4,128)S(1)} %get-tuple-element.1077), channel_id=1, source_target_pairs={{0,32},{32,64},{64,96},{96,0},{1,33},{33,65},{65,97},{97,1},{2,34}... | collective-permute-start | bytes 442376 | tf_op jit(solution)/shard_map/ppermute | solution.py:17
  194.1 15.2 %collective-permute-start.15 = (f32[4,2,3,3,4,1,1,128]{7,0,5,4,3,2,6,1:T(4,128)S(1)}, f32[4,2,3,3,4,1,1,128]{7,0,5,4,3,2,6,1:T(4,128)S(1)}, u32[]{:S(2)}, u32[]{:S(2)}) collective-permute-start(f32[4,2,3,3,4,1,1,128]{7,0,5,4,3,2,6,1:T(4,128)S(1)} %get-tuple-element.1078), channel_id=1, source_target_pairs={{32,0},{64,32},{96,64},{0,96},{33,1},{65,33},{97,65},{1,97},{34,2}... | collective-permute-start | bytes 442376 | tf_op jit(solution)/shard_map/ppermute | solution.py:18
  209.4 43.8 %collective-permute-start.16 = (f32[4,2,3,3,4,4,1,128]{7,0,5,4,3,2,6,1:T(4,128)S(1)}, f32[4,2,3,3,4,4,1,128]{7,0,5,4,3,2,6,1:T(4,128)S(1)}, u32[]{:S(2)}, u32[]{:S(2)}) collective-permute-start(f32[4,2,3,3,4,4,1,128]{7,0,5,4,3,2,6,1:T(4,128)S(1)} %pad_maximum_fusion.5), channel_id=1, source_target_pairs={{0,1},{1,2},{2,3},{3,4},{4,5},{5,6},{6,7},{7,8},{8,9},{9,10},{10,1... | collective-permute-start | bytes 1769480 | tf_op jit(solution)/shard_map/ppermute | solution.py:17
  211.4 41.9 %collective-permute-start.17 = (f32[4,2,3,3,4,4,1,128]{7,0,5,4,3,2,6,1:T(4,128)S(1)}, f32[4,2,3,3,4,4,1,128]{7,0,5,4,3,2,6,1:T(4,128)S(1)}, u32[]{:S(2)}, u32[]{:S(2)}) collective-permute-start(f32[4,2,3,3,4,4,1,128]{7,0,5,4,3,2,6,1:T(4,128)S(1)} %pad_maximum_fusion.5), channel_id=1, source_target_pairs={{1,0},{2,1},{3,2},{4,3},{5,4},{6,5},{7,6},{8,7},{9,8},{10,9},{11,1... | collective-permute-start | bytes 1769480 | tf_op jit(solution)/shard_map/ppermute | solution.py:18
where the time goes:
time: 276 us; the launch traced here: 273 us
  starting transfers between devices  114 us (41%)
  waiting for transfers between devices  56.8 us (21%)
  other arithmetic  53.2 us (19%)
  blocking collectives  22.6 us (8%)
  between operations  14.7 us (5%)
  local copies, waits for them, and re-layouts  11.3 us (4%)
    ppermute x9, starting transfers between devices, padded_2(): after = lax.ppermute(initial, axis, down)  63.3 us
    ppermute x9, starting transfers between devices, padded_2(): before = lax.ppermute(last, axis, up)  51.1 us
    ppermute x9, waiting for transfers between devices, padded_2(): after = lax.ppermute(initial, axis, down)  45.1 us
    reduce_sum x135, other arithmetic, contract(): return jnp.sum(first_part[:, :, None] * second_part[None, :, :], axis=1)  23.8 us
    all_to_all x1, blocking collectives, sent_to_all(): lax.all_to_all(jnp.broadcast_to(shard[None], (devices, *shard.shape)), ax...  22.6 us
    ppermute x9, waiting for transfers between devices, padded_2(): before = lax.ppermute(last, axis, up)  11.7 us
    reduce_sum x12, other arithmetic, flow_force(): jnp.sum(1.0 - trace_real(link_here, upper) / 3.0, axis=(0, 1, 3))  7.56 us
  transfers between devices with their start and end apart: 18, of which 12 were waited for; matrix products, arithmetic and copies ran while one was open for 3% of the time, Pallas kernels for 0%

commit v1 on v0

v1 whole, which is shorter than its diff:
```python
import functools

import jax
import jax.numpy as jnp
from jax import lax
from jax.experimental import pallas as pl
from jax.experimental.pallas import tpu as pltpu
from jax.sharding import PartitionSpec as P


INTERPRET = False

flow_eps = 0.1
X, Y, T, Z = 0, 1, 2, 3
NZ = 128


TWO_ROWS = (0, 1, 2, 3, 4, 5, 9, 10, 11, 12, 13, 14)
TWO_ROWS_CUTS = ((0, 6, 0), (9, 15, 6))
GENERATOR_CUTS = ((1, 3, 0), (5, 6, 2), (10, 12, 3), (14, 15, 5), (9, 10, 6), (13, 14, 7))


def message_form(stage):
    return (12, TWO_ROWS_CUTS, TWO_ROWS) if stage == 0 else (8, GENERATOR_CUTS, tuple(range(18)))


def message_shape(stage):
    faces, _, corners = message_form(stage)
    return (faces + len(corners) // 2, 8, NZ)


def comps(ref, *lead):
    return [ref[(*lead, c)] for c in range(18)]


def times(a, b, b_adjoint=False, a_adjoint=False):
    def ga(i, k):
        return (a[k * 3 + i], a[9 + k * 3 + i]) if a_adjoint else (a[i * 3 + k], a[9 + i * 3 + k])

    def gb(k, j):
        return (b[j * 3 + k], b[9 + j * 3 + k]) if b_adjoint else (b[k * 3 + j], b[9 + k * 3 + j])

    real, imag = [], []
    same = a_adjoint == b_adjoint
    for i in range(3):
        for j in range(3):
            rr = ii = ri = ir = None
            for k in range(3):
                ar, ai = ga(i, k)
                br, bi = gb(k, j)
                rr = ar * br if rr is None else rr + ar * br
                ii = ai * bi if ii is None else ii + ai * bi
                ri = ar * bi if ri is None else ri + ar * bi
                ir = ai * br if ir is None else ir + ai * br
            real.append(rr - ii if same else rr + ii)
            if a_adjoint:
                imag.append(ri - ir if not b_adjoint else -(ri + ir))
            else:
                imag.append(ri + ir if not b_adjoint else ir - ri)
    return real + imag


def put(ref, values, *lead):
    for c in range(18):
        ref[(*lead, c)] = values[c]


def roll_rows(v, shift):
    return pltpu.roll(v, shift, 0)


def roll_lanes(v, shift):
    return pltpu.roll(v, shift % NZ, 1)


def expo_times(x, w):
    x2 = times(x, x)
    x3 = times(x2, x)
    q = [x[c] * (1.0 / 24.0) + x2[c] * (1.0 / 120.0) + x3[c] * (1.0 / 720.0) for c in range(18)]
    r = times(x3, q)
    for c in range(18):
        r[c] = r[c] + (x[c] + x2[c] * 0.5 + x3[c] * (1.0 / 6.0))
    for c in (0, 4, 8):
        r[c] = r[c] + 1.0
    return times(r, w)


def third_row(ref, rows):
    for k, (i, j) in enumerate(((1, 2), (2, 0), (0, 1))):
        ari, aii, arj, aij = ref[i, rows], ref[9 + i, rows], ref[j, rows], ref[9 + j, rows]
        bri, bii, brj, bij = ref[3 + i, rows], ref[12 + i, rows], ref[3 + j, rows], ref[12 + j, rows]
        ref[6 + k, rows] = (ari * brj - aii * bij) - (arj * bri - aij * bii)
        ref[15 + k, rows] = (arj * bii + aij * bri) - (ari * bij + aii * brj)


def unpack_faces(stage, raw_ref, before_ref, full_ref):
    for h in range(raw_ref.shape[1] // 8):
        rows = slice(h * 8, h * 8 + 8)
        if stage == 0:
            for lo, hi, at in TWO_ROWS_CUTS:
                full_ref[lo:hi, rows] = raw_ref[at : at + hi - lo, rows]
            third_row(full_ref, rows)
            continue
        g = [raw_ref[m, rows] for m in range(8)]
        if stage == 1:
            g = [v * 0.25 for v in g]
        r01, r02, r12, i01, i02, i12, d0, d1 = g
        zero = jnp.zeros((8, NZ), jnp.float32)
        x = [zero, r01, r02, -r01, zero, r12, -r02, -r12, zero, d0, i01, i02, i01, d1, i12, i02, i12, -(d0 + d1)]
        new = expo_times(x, [before_ref[c, rows] for c in range(18)])
        for c in range(18):
            full_ref[c, rows] = new[c]


def unpack_corners(stage, raw_ref, full_ref):
    faces, _, corners = message_form(stage)
    for m, c in enumerate(corners):
        row = (m % 2) * 3
        full_ref[c, 8:11] = raw_ref[faces + m // 2, row : row + 3]
    if stage == 0:
        third_row(full_ref, slice(8, 16))


def row_ids(rows):
    return lax.broadcasted_iota(jnp.int32, (rows, NZ), 0)


def lane_ids(rows):
    return lax.broadcasted_iota(jnp.int32, (rows, NZ), 1)


def is_even(where_ref, k):
    return where_ref[k] % 2 == 0


def sort_pair(even, a_ref, b_ref, plus_ref, minus_ref):
    mask = jnp.broadcast_to(even, a_ref.shape[1:])
    for c in range(plus_ref.shape[0]):
        a, b = a_ref[c], b_ref[c]
        plus_ref[c] = jnp.where(mask, a, b)
        minus_ref[c] = jnp.where(mask, b, a)


def stage_kernel(stage, where_ref, s_ref, xp_ref, xm_ref, tp_ref, tm_ref, ya_ref, yb_ref, qa_ref, qb_ref, *rest):
    rest = list(rest)
    z_ref = rest.pop(0) if stage else None
    before = (rest.pop(0), rest.pop(0)) if stage else (None, None)
    act_ref = rest.pop(0) if stage == 1 else None
    s_out = rest.pop(0)
    if stage < 2:
        xa_out, xb_out, hop_out = rest.pop(0), rest.pop(0), rest.pop(0)
        z_out = rest.pop(0)
        act_out = rest.pop(0)
        plus_out, minus_out = rest.pop(0), rest.pop(0)
    v_ref, r_ref, t_ref, b_ref, u_ref, w_ref, g_ref = rest[:7]
    yp_ref, ym_ref, qp_ref, qm_ref, yp_raw, ym_raw, yp_face, ym_face = rest[7:]
    sort_pair(is_even(where_ref, 1), ya_ref, yb_ref, yp_raw, ym_raw)
    sort_pair(is_even(where_ref, 2), qa_ref, qb_ref, qp_ref, qm_ref)
    for k, (raw, face, full) in enumerate(((yp_raw, yp_face, yp_ref), (ym_raw, ym_face, ym_ref))):
        unpack_faces(stage, raw, before[k], face)
        full[:, 0:8] = face[...]
        unpack_corners(stage, raw, full)
    if stage < 2:
        plus_out[...] = yp_face[...]
        minus_out[...] = ym_face[...]

    own = lambda d: slice(d * 4, d * 4 + 4)
    for nu in range(4):
        for mu in range(4):
            v_ref[nu, mu, :, 0:4] = s_ref[:, own(mu)]
            if nu == X:
                v_ref[nu, mu, :, 6:8] = xm_ref[:, mu * 2 : mu * 2 + 2]
            elif nu == Y:
                v_ref[nu, mu, :, 7:8] = ym_ref[0:18, mu * 2 : mu * 2 + 1]
                v_ref[nu, mu, :, 5:6] = ym_ref[0:18, mu * 2 + 1 : mu * 2 + 2]
            elif nu == T:
                v_ref[nu, mu, :, 4:8] = tm_ref[:, own(mu)]
    for nu in range(4):
        if nu != X:
            r_ref[nu, X, :, 0:2] = s_ref[:, nu * 4 + 2 : nu * 4 + 4]
            r_ref[nu, X, :, 2:4] = xp_ref[:, nu * 2 : nu * 2 + 2]
        if nu != Y:
            r_ref[nu, Y, :, 0:1] = s_ref[:, nu * 4 + 1 : nu * 4 + 2]
            r_ref[nu, Y, :, 1:2] = yp_ref[0:18, nu * 2 : nu * 2 + 1]
            r_ref[nu, Y, :, 2:3] = s_ref[:, nu * 4 + 3 : nu * 4 + 4]
            r_ref[nu, Y, :, 3:4] = yp_ref[0:18, nu * 2 + 1 : nu * 2 + 2]
        if nu != T:
            r_ref[nu, T, :, 0:4] = tp_ref[:, own(nu)]
        if nu != Z:
            for c in range(18):
                r_ref[nu, Z, c] = roll_lanes(v_ref[nu, nu, c], -1)
    r_ref[X, Y, :, 6:7] = xm_ref[:, 1:2]
    r_ref[X, Y, :, 7:8] = yp_ref[0:18, 8:9]
    r_ref[X, T, :, 6:8] = qp_ref[...]
    r_ref[Y, X, :, 7:8] = ym_ref[0:18, 3:4]
    r_ref[Y, X, :, 5:6] = ym_ref[0:18, 8:9]
    r_ref[Y, T, :, 7:8] = ym_ref[0:18, 9:10]
    r_ref[Y, T, :, 5:6] = ym_ref[0:18, 10:11]
    r_ref[T, X, :, 4:6] = tm_ref[:, 10:12]
    r_ref[T, X, :, 6:8] = qm_ref[...]
    r_ref[T, Y, :, 4:5] = tm_ref[:, 9:10]
    r_ref[T, Y, :, 5:6] = yp_ref[0:18, 9:10]
    r_ref[T, Y, :, 6:7] = tm_ref[:, 11:12]
    r_ref[T, Y, :, 7:8] = yp_ref[0:18, 10:11]

    for mu in range(4):
        for c in range(18):
            b_ref[mu, c] = jnp.zeros((8, NZ), jnp.float32)
            u_ref[mu, c] = jnp.zeros((8, NZ), jnp.float32)
    rows = row_ids(8)
    for nu in range(4):

        def lower(m, carry, nu=nu):
            mu = m + (m >= nu).astype(jnp.int32)
            t = times(comps(v_ref, nu, mu), comps(r_ref, nu, mu))
            put(t_ref, t, nu, mu)
            low = times(t, comps(v_ref, nu, nu), a_adjoint=True)
            for c in range(18):
                v = low[c]
                if nu == X:
                    v = roll_rows(v, 2)
                elif nu == Y:
                    v = jnp.where(rows == 2, roll_rows(v, 5), roll_rows(v, 1))
                elif nu == T:
                    v = roll_rows(v, 4)
                else:
                    v = roll_lanes(v, 1)
                b_ref[mu, c] = b_ref[mu, c] + v
            return carry

        lax.fori_loop(0, 3, lower, 0)

    trace = None
    for mu in range(4):
        for nu in range(mu + 1, 4):
            p = times(comps(t_ref, nu, mu), comps(t_ref, mu, nu), b_adjoint=True)
            for i in range(3):
                for j in range(3):
                    k, l = i * 3 + j, j * 3 + i
                    u_ref[mu, k] = u_ref[mu, k] + p[k]
                    u_ref[mu, 9 + k] = u_ref[mu, 9 + k] + p[9 + k]
                    u_ref[nu, k] = u_ref[nu, k] + p[l]
                    u_ref[nu, 9 + k] = u_ref[nu, 9 + k] - p[9 + l]
            if stage == 0:
                part = 1.0 - (p[0] + p[4] + p[8]) / 3.0
                trace = part if trace is None else trace + part

    def force(mu, carry):
        omega = times(comps(v_ref, 3, mu), comps(b_ref, mu))
        omega = [omega[c] + u_ref[mu, c] for c in range(18)]
        mean = (omega[9] + omega[13] + omega[17]) / 3.0
        for i in range(3):
            for j in range(3):
                k, l = i * 3 + j, j * 3 + i
                g_ref[mu, k] = (-0.5 * flow_eps) * (omega[k] - omega[l])
                imag = 0.5 * (omega[9 + k] + omega[9 + l])
                if i == j:
                    imag = imag - mean
                g_ref[mu, 9 + k] = -flow_eps * imag
        return carry

    lax.fori_loop(0, 4, force, 0)
    for mu in range(4):
        w_ref[mu // 2, :, (mu % 2) * 4 : (mu % 2) * 4 + 4] = g_ref[mu, :, 0:4]

    for h in range(2):
        x = comps(w_ref, h)
        half = slice(h * 8, h * 8 + 8)
        if stage == 0:
            for c in range(18):
                z_out[c, half] = x[c]
            x = [v * 0.25 for v in x]
        elif stage == 1:
            x = [x[c] * (8.0 / 9.0) - z_ref[c, half] * (17.0 / 36.0) for c in range(18)]
            for c in range(18):
                z_out[c, half] = x[c]
        else:
            x = [x[c] * 0.75 - z_ref[c, half] for c in range(18)]
        new = expo_times(x, [s_ref[c, half] for c in range(18)])
        for c in range(18):
            if stage < 2:
                s_out[c, half] = new[c]
            else:
                s_out[h * 2, c] = new[c][0:4]
                s_out[h * 2 + 1, c] = new[c][4:8]

    if stage < 2:
        if stage == 0:
            total = jnp.sum(jnp.where(rows < 4, trace, 0.0))
            mine = where_ref[0] * 4 + where_ref[1]
            act = jnp.where(lane_ids(8) == mine, jnp.broadcast_to(total, (8, NZ)), 0.0)
        else:
            known = ya_ref[8, 6:7] + yb_ref[8, 6:7]
            act = act_ref[...] + jnp.broadcast_to(known, (8, NZ))
        act_out[...] = act
        fill_faces(stage + 1, where_ref, z_out, act, xa_out, xb_out, hop_out)


def fill_faces(stage, where_ref, from_ref, act, xa_out, xb_out, hop_out):
    faces, cuts, _ = message_form(stage)

    def fill(hi_out, lo_out):
        for lo, hi, at in cuts:
            to = slice(at, at + hi - lo)
            for d in range(4):
                hi_out[to, d * 2 : d * 2 + 2] = from_ref[lo:hi, d * 4 + 2 : d * 4 + 4]
                lo_out[to, d * 2 : d * 2 + 2] = from_ref[lo:hi, d * 4 : d * 4 + 2]
        hi_out[faces] = act
        lo_out[faces] = act

    even = is_even(where_ref, 0)
    pl.when(even)(lambda: fill(xa_out, xb_out))
    pl.when(jnp.logical_not(even))(lambda: fill(xb_out, xa_out))
    for lo, hi, at in cuts:
        hop_out[at : at + hi - lo] = from_ref[lo:hi]


def first_kernel(where_ref, l_ref, s_out, xa_out, xb_out, hop_out):
    for d in range(4):
        s_out[:, d * 4 : d * 4 + 4] = l_ref[d]
    fill_faces(0, where_ref, s_out, jnp.zeros((8, NZ), jnp.float32), xa_out, xb_out, hop_out)


def pack_kernel(stage, where_ref, s_ref, xa_ref, xb_ref, ta_ref, tb_ref, act_ref, *rest):
    rest = list(rest)
    before = [rest.pop(0) for _ in range(4)] if stage else [None] * 4
    ya_out, yb_out, qa_out, qb_out, act_out, xp_ref, xm_ref, tp_ref, tm_ref = rest[:9]
    xp_raw, xm_raw, tp_raw, tm_raw = rest[9:]
    even_x, even_y, even_t = (is_even(where_ref, k) for k in range(3))
    faces, cuts, corners = message_form(stage)
    sort_pair(even_x, xa_ref, xb_ref, xp_raw, xm_raw)
    sort_pair(even_t, ta_ref, tb_ref, tp_raw, tm_raw)
    for k, (raw, full) in enumerate(((xp_raw, xp_ref), (xm_raw, xm_ref), (tp_raw, tp_ref), (tm_raw, tm_ref))):
        unpack_faces(stage, raw, before[k], full)

    act = act_ref[...]
    from_plus, from_minus = xp_raw[faces], xm_raw[faces]
    if stage == 1:
        act = act + from_plus + from_minus
    elif stage == 2:
        gx = lane_ids(8) // 4
        plus = gx == (where_ref[0] + 2) % 8
        minus = gx == (where_ref[0] + 6) % 8
        act = act + jnp.where(plus, from_plus, 0.0) + jnp.where(minus, from_minus, 0.0)
    act_out[...] = act

    hi_corner = ((xp_ref, 3), (tp_ref, 5), (tp_ref, 7))
    lo_corner = ((xm_ref, 0), (tm_ref, 8), (tm_ref, 10))

    def fill_y(hi_out, lo_out):
        for d in range(4):
            for x in range(2):
                k = d * 2 + x
                r = d * 4 + x * 2
                for lo, hi, at in cuts:
                    hi_out[at : at + hi - lo, k : k + 1] = s_ref[lo:hi, r + 1 : r + 2]
                    lo_out[at : at + hi - lo, k : k + 1] = s_ref[lo:hi, r : r + 1]
        for out, corner in ((hi_out, hi_corner), (lo_out, lo_corner)):
            for m, c in enumerate(corners):
                for k, (ref, at) in enumerate(corner):
                    row = (m % 2) * 3 + k
                    out[faces + m // 2, row : row + 1] = ref[c, at : at + 1]
            out[faces, 6:7] = act[0:1]

    pl.when(even_y)(lambda: fill_y(ya_out, yb_out))
    pl.when(jnp.logical_not(even_y))(lambda: fill_y(yb_out, ya_out))

    hi = xp_ref[:, T * 2 : T * 2 + 2]
    lo = xm_ref[:, X * 2 : X * 2 + 2]
    mask_t = jnp.broadcast_to(even_t, (18, 2, NZ))
    qa_out[...] = jnp.where(mask_t, hi, lo)
    qb_out[...] = jnp.where(mask_t, lo, hi)


VM = pl.BlockSpec(memory_space=pltpu.VMEM)
SM = pl.BlockSpec(memory_space=pltpu.SMEM)


def arr(*shape):
    return jax.ShapeDtypeStruct(shape, jnp.float32)


def x_message(stage):
    return arr(message_form(stage)[0] + 1, 8, NZ)


def t_message(stage):
    return arr(message_form(stage)[0], 16, NZ)


def call(kernel, outs, scratch, where, *args):
    return pl.pallas_call(
        kernel,
        out_shape=outs,
        in_specs=[SM] + [VM] * len(args),
        out_specs=[VM] * len(outs),
        scratch_shapes=[pltpu.VMEM((*s, NZ), jnp.float32) for s in scratch],
        interpret=INTERPRET,
        compiler_params=pltpu.CompilerParams(vmem_limit_bytes=16 * 2**20),
    )(where, *args)


def run_stage(stage, *args):
    outs = [arr(18, 16, NZ)] if stage < 2 else [arr(4, 18, 4, NZ)]
    if stage < 2:
        outs += [x_message(stage + 1), x_message(stage + 1), t_message(stage + 1)]
        outs += [arr(18, 16, NZ), arr(8, NZ), arr(18, 8, NZ), arr(18, 8, NZ)]
    scratch = [(4, 4, 18, 8), (4, 4, 18, 8), (4, 4, 18, 8), (4, 18, 8), (4, 18, 8), (2, 18, 8), (4, 18, 8)]
    scratch += [(18, 16), (18, 16), (18, 2), (18, 2)] + [message_shape(stage)[:2]] * 2 + [(18, 8), (18, 8)]
    return call(functools.partial(stage_kernel, stage), outs, scratch, *args)


def run_pack(stage, *args):
    outs = [arr(*message_shape(stage))] * 2 + [arr(18, 2, NZ)] * 2 + [arr(8, NZ)]
    outs += [arr(18, 8, NZ)] * 2 + [arr(18, 16, NZ)] * 2
    faces = message_form(stage)[0]
    scratch = [(faces + 1, 8)] * 2 + [(faces, 16)] * 2
    return call(functools.partial(pack_kernel, stage), outs, scratch, *args)


def run_first(where, links):
    outs = [arr(18, 16, NZ), x_message(0), x_message(0), t_message(0)]
    return call(first_kernel, outs, [], where, links)


def swap(value, axis, odd):
    n = lax.axis_size(axis)
    return lax.ppermute(value, axis, [(i, (((i + odd) ^ 1) - odd) % n) for i in range(n)])


def steps(links):
    where = jnp.stack([lax.axis_index(a) for a in ("gx", "gy", "ta")]).astype(jnp.int32)
    state, xa, xb, hop = run_first(where, links.reshape(4, 18, 4, NZ))
    act = jnp.zeros((8, NZ), jnp.float32)
    kept = None
    for k in range(3):
        xb = swap(xb, "gx", 1)
        xa = swap(xa, "gx", 0)
        tb = swap(hop, "ta", 1)
        ta = swap(hop, "ta", 0)
        packed = run_pack(k, where, kept if k else state, xa, xb, ta, tb, act, *(sides if k else ()))
        ya, yb, qa, qb, act, *sides = packed
        yb = swap(yb, "gy", 1)
        qb = swap(qb, "ta", 1)
        qa = swap(qa, "ta", 0)
        ya = swap(ya, "gy", 0)
        halo = (*sides, ya, yb, qa, qb)
        if k == 0:
            state, xa, xb, hop, kept, act, *before = run_stage(0, where, state, *halo)
        elif k == 1:
            state, xa, xb, hop, kept, act, *before = run_stage(1, where, state, *halo, kept, *before, act)
        else:
            lane = jnp.arange(NZ)
            far_y = lane % 4 == (where[1] + 2) % 4
            act = act[0] + jnp.where(far_y, ya[8, 6], 0.0)
            other = lax.ppermute(act, "gx", [(i, (i + 4) % 8) for i in range(8)])
            state = run_stage(2, where, state, *halo, kept, *before)[0]
            near_x = (lane // 4 - where[0] + 2) % 8 < 5
            act = jnp.where(near_x, act, other)
    flowed = state.reshape(links.shape)
    sites_slice = 6.0 * links.shape[4] * lax.axis_size("gx") * links.shape[5] * lax.axis_size("gy") * links.shape[7]
    return (flowed, (jnp.sum(act[:32]) / sites_slice).reshape(1))


def solution(mesh):
    spec = P(None, None, None, None, "gx", "gy", "ta", None)
    return jax.shard_map(steps, mesh=mesh, in_specs=(spec,), out_specs=(spec, P("ta")), check_vma=False)
```

time: 276 us -> 168 us (0.61)
  other arithmetic: 53.2 us -> 0.7 us
  waiting for transfers between devices: 56.8 us -> 24.6 us
  blocking collectives: 22.6 us -> 0 us
  Pallas kernels: 0 us -> 14.1 us
  between operations: 14.7 us -> 2.75 us
  local copies, waits for them, and re-layouts: 11.3 us -> 0.91 us
  starting transfers between devices: 114 us -> 124 us
    ppermute x18 -> x25, waiting for transfers between devices: 56.8 us -> 24.6 us  [the longest x24 24.6 us: swap(): lax.ppermute(value, axis, [(i, ((i + odd ^ 1) - odd) % n) for i in range(...]
    reduce_sum x155 -> x1, other arithmetic: 32.6 us -> 0.6 us  [steps(): return (flowed, (jnp.sum(act[:32]) / sites_slice).reshape(1))]
    all_to_all x1 -> x0, blocking collectives: 22.6 us -> none  [sent_to_all(): lax.all_to_all(jnp.broadcast_to(shard[None], (devices, *shard.shape)), ax...]
    pallas_call x0 -> x7, Pallas kernels: none -> 14.1 us  [call(): pl.pallas_call(kernel, out_shape=outs, in_specs=[SM] + [VM] * len(args),...]
    ppermute x18 -> x25, starting transfers between devices: 114 us -> 124 us  [the longest x24 122 us: swap(): lax.ppermute(value, axis, [(i, ((i + odd ^ 1) - odd) % n) for i in range(...]
    slice x32 -> x0, local copies, waits for them, and re-layouts: 7.79 us -> none  [the longest x20 3.49 us: shifted(): view = jnp.roll(view, -offset[3], axis=-1)]
    concatenate x15 -> x0, other arithmetic: 4.89 us -> none  [the longest x8 3.88 us: padded_2(): shard = jnp.concatenate([before, shard, after], axis=dim)]
    mul x36 -> x0, other arithmetic: 4.04 us -> none  [the longest x34 3.9 us: contract(): return jnp.sum(first_part[:, :, None] * second_part[None, :, :], axis=1)]
  transfers between devices with their start and end apart: 18 -> 25, of which waited for: 12 -> 6; matrix products, arithmetic and copies ran while one was open for 3% -> 0% of each run, Pallas kernels for 0% -> 2%
where the time goes in v1:
time: 168 us; the launch traced here: 167 us
  starting transfers between devices  124 us (74%)
  waiting for transfers between devices  24.6 us (15%)
  Pallas kernels  14.1 us (8%)
  between operations  2.75 us (2%)
    ppermute x24, starting transfers between devices, swap(): lax.ppermute(value, axis, [(i, ((i + odd ^ 1) - odd) % n) for i in range(...  122 us
    ppermute x24, waiting for transfers between devices, swap(): lax.ppermute(value, axis, [(i, ((i + odd ^ 1) - odd) % n) for i in range(...  24.6 us
    pallas_call x7, Pallas kernels, call(): pl.pallas_call(kernel, out_shape=outs, in_specs=[SM] + [VM] * len(args),...  14.1 us
  transfers between devices with their start and end apart: 25, of which 6 were waited for; matrix products, arithmetic and copies ran while one was open for 0% of the time, Pallas kernels for 2%

profile of v1, /device:TPU:1, one launch (start us, length us, event | category | flops | bytes accessed | tf_op | source)
XLA Modules:
  0.0 166.9 jit_solution(17118320734483106542)
XLA Ops:
  0.6 0.1 pad_add_fusion.where_ref
  0.7 0.9 copy-done
  1.6 0.6 shard_map.30
  2.2 8.1 %collective-permute-start.3 = (f32[12,16,128]{2,1,0:T(8,128)S(1)}, f32[12,16,128]{2,1,0:T(8,128)S(1)}, u32[]{:S(2)}, u32[]{:S(2)}) collective-permute-start(f32[12,16,128]{2,1,0:T(8,128)S(1)} %get-tuple-element.51), channel_id=1, source_target_pairs={{0,31},{1,2},{2,1},{3,4},{4,3},{5,6},{6,5},{7,8},{8,7},{9,10},{10,... | collective-permute-start | bytes 294920 | tf_op jit(solution)/shard_map/ppermute | solution.py:428
  10.4 1.9 %collective-permute-start.2 = (f32[12,16,128]{2,1,0:T(8,128)S(1)}, f32[12,16,128]{2,1,0:T(8,128)S(1)}, u32[]{:S(2)}, u32[]{:S(2)}) collective-permute-start(f32[12,16,128]{2,1,0:T(8,128)S(1)} %get-tuple-element.51), channel_id=1, source_target_pairs={{0,1},{1,0},{2,3},{3,2},{4,5},{5,4},{6,7},{7,6},{8,9},{9,8},{10,11... | collective-permute-start | bytes 294920 | tf_op jit(solution)/shard_map/ppermute | solution.py:428
  12.3 4.0 %collective-permute-start = (f32[13,8,128]{2,1,0:T(8,128)S(1)}, f32[13,8,128]{2,1,0:T(8,128)S(1)}, u32[]{:S(2)}, u32[]{:S(2)}) collective-permute-start(f32[13,8,128]{2,1,0:T(8,128)S(1)} %get-tuple-element.49), channel_id=1, source_target_pairs={{0,128},{128,0},{256,384},{384,256},{512,640},{640,512},{768,896},... | collective-permute-start | bytes 159752 | tf_op jit(solution)/shard_map/ppermute | solution.py:428
  16.3 14.0 %collective-permute-start.1 = (f32[13,8,128]{2,1,0:T(8,128)S(1)}, f32[13,8,128]{2,1,0:T(8,128)S(1)}, u32[]{:S(2)}, u32[]{:S(2)}) collective-permute-start(f32[13,8,128]{2,1,0:T(8,128)S(1)} %get-tuple-element.50), channel_id=1, source_target_pairs={{0,896},{128,256},{256,128},{384,512},{512,384},{640,768},{768,640... | collective-permute-start | bytes 159752 | tf_op jit(solution)/shard_map/ppermute | solution.py:428
  30.3 1.5 collective-permute-done.1.xb_ref
  31.8 0.0 collective-permute-done.3.tb_ref
  31.8 0.0 collective-permute-done.2.ta_ref
  31.8 1.3 shard_map.31
  33.2 4.8 %collective-permute-start.4 = (f32[18,8,128]{2,1,0:T(8,128)S(1)}, f32[18,8,128]{2,1,0:T(8,128)S(1)}, u32[]{:S(2)}, u32[]{:S(2)}) collective-permute-start(f32[18,8,128]{2,1,0:T(8,128)S(1)} %get-tuple-element.56), channel_id=1, source_target_pairs={{0,32},{32,0},{64,96},{96,64},{1,33},{33,1},{65,97},{97,65},{2,34}... | collective-permute-start | bytes 221192 | tf_op jit(solution)/shard_map/ppermute | solution.py:428
  38.0 13.5 %collective-permute-start.5 = (f32[18,8,128]{2,1,0:T(8,128)S(1)}, f32[18,8,128]{2,1,0:T(8,128)S(1)}, u32[]{:S(2)}, u32[]{:S(2)}) collective-permute-start(f32[18,8,128]{2,1,0:T(8,128)S(1)} %get-tuple-element.57), channel_id=1, source_target_pairs={{0,96},{32,64},{64,32},{96,0},{1,97},{33,65},{65,33},{97,1},{2,98}... | collective-permute-start | bytes 221192 | tf_op jit(solution)/shard_map/ppermute | solution.py:428
  51.5 3.6 %collective-permute-start.6 = (f32[18,2,128]{2,1,0:T(2,128)S(1)}, f32[18,2,128]{2,1,0:T(2,128)S(1)}, u32[]{:S(2)}, u32[]{:S(2)}) collective-permute-start(f32[18,2,128]{2,1,0:T(2,128)S(1)} %get-tuple-element.58), channel_id=1, source_target_pairs={{0,1},{1,0},{2,3},{3,2},{4,5},{5,4},{6,7},{7,6},{8,9},{9,8},{10,11... | collective-permute-start | bytes 55304 | tf_op jit(solution)/shard_map/ppermute | solution.py:428
  55.1 2.6 %collective-permute-start.7 = (f32[18,2,128]{2,1,0:T(2,128)S(1)}, f32[18,2,128]{2,1,0:T(2,128)S(1)}, u32[]{:S(2)}, u32[]{:S(2)}) collective-permute-start(f32[18,2,128]{2,1,0:T(2,128)S(1)} %get-tuple-element.59), channel_id=1, source_target_pairs={{0,31},{1,2},{2,1},{3,4},{4,3},{5,6},{6,5},{7,8},{8,7},{9,10},{10,... | collective-permute-start | bytes 55304 | tf_op jit(solution)/shard_map/ppermute | solution.py:428
  57.7 5.2 %collective-permute-done.7.qb_ref = f32[18,2,128]{2,1,0:T(2,128)S(1)} collective-permute-done((f32[18,2,128]{2,1,0:T(2,128)S(1)}, f32[18,2,128]{2,1,0:T(2,128)S(1)}, u32[]{:S(2)}, u32[]{:S(2)}) %collective-permute-start.7) | collective-permute-done | bytes 18464 | tf_op jit(solution)/shard_map/ppermute | solution.py:428
  63.0 0.0 collective-permute-done.4.ya_ref
  63.0 0.0 collective-permute-done.5.yb_ref
  63.0 2.9 %shard_map.32 = (f32[18,16,128]{2,1,0:T(8,128)S(1)}, f32[9,8,128]{2,1,0:T(8,128)S(1)}, f32[9,8,128]{2,1,0:T(8,128)S(1)}, f32[8,16,128]{2,1,0:T(8,128)S(1)}, f32[...) custom-call(s32[3]{0:T(128)S(1)} %pad_add_fusion.where_ref, ...), custom_call_target="tpu_custom_call" | custom-call | tf_op jit(solution)/shard_map/pallas_call | solution.py:392
  65.8 2.6 %collective-permute-start.11 = (f32[8,16,128]{2,1,0:T(8,128)S(1)}, f32[8,16,128]{2,1,0:T(8,128)S(1)}, u32[]{:S(2)}, u32[]{:S(2)}) collective-permute-start(f32[8,16,128]{2,1,0:T(8,128)S(1)} %get-tuple-element.64), channel_id=1, source_target_pairs={{0,31},{1,2},{2,1},{3,4},{4,3},{5,6},{6,5},{7,8},{8,7},{9,10},{10,... | collective-permute-start | bytes 196616 | tf_op jit(solution)/shard_map/ppermute | solution.py:428
  68.4 1.9 %collective-permute-start.10 = (f32[8,16,128]{2,1,0:T(8,128)S(1)}, f32[8,16,128]{2,1,0:T(8,128)S(1)}, u32[]{:S(2)}, u32[]{:S(2)}) collective-permute-start(f32[8,16,128]{2,1,0:T(8,128)S(1)} %get-tuple-element.64), channel_id=1, source_target_pairs={{0,1},{1,0},{2,3},{3,2},{4,5},{5,4},{6,7},{7,6},{8,9},{9,8},{10,11... | collective-permute-start | bytes 196616 | tf_op jit(solution)/shard_map/ppermute | solution.py:428
  70.4 1.9 %collective-permute-start.8 = (f32[9,8,128]{2,1,0:T(8,128)S(1)}, f32[9,8,128]{2,1,0:T(8,128)S(1)}, u32[]{:S(2)}, u32[]{:S(2)}) collective-permute-start(f32[9,8,128]{2,1,0:T(8,128)S(1)} %get-tuple-element.62), channel_id=1, source_target_pairs={{0,128},{128,0},{256,384},{384,256},{512,640},{640,512},{768,896},... | collective-permute-start | bytes 110600 | tf_op jit(solution)/shard_map/ppermute | solution.py:428
  72.3 7.7 %collective-permute-start.9 = (f32[9,8,128]{2,1,0:T(8,128)S(1)}, f32[9,8,128]{2,1,0:T(8,128)S(1)}, u32[]{:S(2)}, u32[]{:S(2)}) collective-permute-start(f32[9,8,128]{2,1,0:T(8,128)S(1)} %get-tuple-element.63), channel_id=1, source_target_pairs={{0,896},{128,256},{256,128},{384,512},{512,384},{640,768},{768,640... | collective-permute-start | bytes 110600 | tf_op jit(solution)/shard_map/ppermute | solution.py:428
  80.0 3.6 %collective-permute-done.9.xb_ref = f32[9,8,128]{2,1,0:T(8,128)S(1)} collective-permute-done((f32[9,8,128]{2,1,0:T(8,128)S(1)}, f32[9,8,128]{2,1,0:T(8,128)S(1)}, u32[]{:S(2)}, u32[]{:S(2)}) %collective-permute-start.9) | collective-permute-done | bytes 36896 | tf_op jit(solution)/shard_map/ppermute | solution.py:428
  83.6 1.4 shard_map.33
  85.0 5.0 %collective-permute-start.12 = (f32[17,8,128]{2,1,0:T(8,128)S(1)}, f32[17,8,128]{2,1,0:T(8,128)S(1)}, u32[]{:S(2)}, u32[]{:S(2)}) collective-permute-start(f32[17,8,128]{2,1,0:T(8,128)S(1)} %get-tuple-element.70), channel_id=1, source_target_pairs={{0,32},{32,0},{64,96},{96,64},{1,33},{33,1},{65,97},{97,65},{2,34}... | collective-permute-start | bytes 208904 | tf_op jit(solution)/shard_map/ppermute | solution.py:428
  90.0 5.0 %collective-permute-start.13 = (f32[17,8,128]{2,1,0:T(8,128)S(1)}, f32[17,8,128]{2,1,0:T(8,128)S(1)}, u32[]{:S(2)}, u32[]{:S(2)}) collective-permute-start(f32[17,8,128]{2,1,0:T(8,128)S(1)} %get-tuple-element.71), channel_id=1, source_target_pairs={{0,96},{32,64},{64,32},{96,0},{1,97},{33,65},{65,33},{97,1},{2,98}... | collective-permute-start | bytes 208904 | tf_op jit(solution)/shard_map/ppermute | solution.py:428
  95.0 3.6 %collective-permute-start.14 = (f32[18,2,128]{2,1,0:T(2,128)S(1)}, f32[18,2,128]{2,1,0:T(2,128)S(1)}, u32[]{:S(2)}, u32[]{:S(2)}) collective-permute-start(f32[18,2,128]{2,1,0:T(2,128)S(1)} %get-tuple-element.72), channel_id=1, source_target_pairs={{0,1},{1,0},{2,3},{3,2},{4,5},{5,4},{6,7},{7,6},{8,9},{9,8},{10,11... | collective-permute-start | bytes 55304 | tf_op jit(solution)/shard_map/ppermute | solution.py:428
  98.6 3.3 %collective-permute-start.15 = (f32[18,2,128]{2,1,0:T(2,128)S(1)}, f32[18,2,128]{2,1,0:T(2,128)S(1)}, u32[]{:S(2)}, u32[]{:S(2)}) collective-permute-start(f32[18,2,128]{2,1,0:T(2,128)S(1)} %get-tuple-element.73), channel_id=1, source_target_pairs={{0,31},{1,2},{2,1},{3,4},{4,3},{5,6},{6,5},{7,8},{8,7},{9,10},{10,... | collective-permute-start | bytes 55304 | tf_op jit(solution)/shard_map/ppermute | solution.py:428
  102.0 4.5 %collective-permute-done.15.qb_ref = f32[18,2,128]{2,1,0:T(2,128)S(1)} collective-permute-done((f32[18,2,128]{2,1,0:T(2,128)S(1)}, f32[18,2,128]{2,1,0:T(2,128)S(1)}, u32[]{:S(2)}, u32[]{:S(2)}) %collective-permute-start.15) | collective-permute-done | bytes 18464 | tf_op jit(solution)/shard_map/ppermute | solution.py:428
  106.5 0.0 collective-permute-done.12.ya_ref
  106.5 0.0 collective-permute-done.13.yb_ref
  106.5 2.9 %shard_map.34 = (f32[18,16,128]{2,1,0:T(8,128)S(1)}, f32[9,8,128]{2,1,0:T(8,128)S(1)}, f32[9,8,128]{2,1,0:T(8,128)S(1)}, f32[8,16,128]{2,1,0:T(8,128)S(1)}, f32[...) custom-call(s32[3]{0:T(128)S(1)} %pad_add_fusion.where_ref, ...), custom_call_target="tpu_custom_call" | custom-call | tf_op jit(solution)/shard_map/pallas_call | solution.py:392
  109.4 4.3 %collective-permute-start.19 = (f32[8,16,128]{2,1,0:T(8,128)S(1)}, f32[8,16,128]{2,1,0:T(8,128)S(1)}, u32[]{:S(2)}, u32[]{:S(2)}) collective-permute-start(f32[8,16,128]{2,1,0:T(8,128)S(1)} %get-tuple-element.81), channel_id=1, source_target_pairs={{0,31},{1,2},{2,1},{3,4},{4,3},{5,6},{6,5},{7,8},{8,7},{9,10},{10,... | collective-permute-start | bytes 196616 | tf_op jit(solution)/shard_map/ppermute | solution.py:428
  113.7 1.9 %collective-permute-start.18 = (f32[8,16,128]{2,1,0:T(8,128)S(1)}, f32[8,16,128]{2,1,0:T(8,128)S(1)}, u32[]{:S(2)}, u32[]{:S(2)}) collective-permute-start(f32[8,16,128]{2,1,0:T(8,128)S(1)} %get-tuple-element.81), channel_id=1, source_target_pairs={{0,1},{1,0},{2,3},{3,2},{4,5},{5,4},{6,7},{7,6},{8,9},{9,8},{10,11... | collective-permute-start | bytes 196616 | tf_op jit(solution)/shard_map/ppermute | solution.py:428
  115.7 1.9 %collective-permute-start.16 = (f32[9,8,128]{2,1,0:T(8,128)S(1)}, f32[9,8,128]{2,1,0:T(8,128)S(1)}, u32[]{:S(2)}, u32[]{:S(2)}) collective-permute-start(f32[9,8,128]{2,1,0:T(8,128)S(1)} %get-tuple-element.79), channel_id=1, source_target_pairs={{0,128},{128,0},{256,384},{384,256},{512,640},{640,512},{768,896},... | collective-permute-start | bytes 110600 | tf_op jit(solution)/shard_map/ppermute | solution.py:428
  117.6 7.7 %collective-permute-start.17 = (f32[9,8,128]{2,1,0:T(8,128)S(1)}, f32[9,8,128]{2,1,0:T(8,128)S(1)}, u32[]{:S(2)}, u32[]{:S(2)}) collective-permute-start(f32[9,8,128]{2,1,0:T(8,128)S(1)} %get-tuple-element.80), channel_id=1, source_target_pairs={{0,896},{128,256},{256,128},{384,512},{512,384},{640,768},{768,640... | collective-permute-start | bytes 110600 | tf_op jit(solution)/shard_map/ppermute | solution.py:428
  125.3 3.6 %collective-permute-done.17.xb_ref = f32[9,8,128]{2,1,0:T(8,128)S(1)} collective-permute-done((f32[9,8,128]{2,1,0:T(8,128)S(1)}, f32[9,8,128]{2,1,0:T(8,128)S(1)}, u32[]{:S(2)}, u32[]{:S(2)}) %collective-permute-start.17) | collective-permute-done | bytes 36896 | tf_op jit(solution)/shard_map/ppermute | solution.py:428
  128.9 0.0 collective-permute-done.19.tb_ref
  128.9 1.4 shard_map.35
  130.3 3.8 %collective-permute-start.20 = (f32[17,8,128]{2,1,0:T(8,128)S(1)}, f32[17,8,128]{2,1,0:T(8,128)S(1)}, u32[]{:S(2)}, u32[]{:S(2)}) collective-permute-start(f32[17,8,128]{2,1,0:T(8,128)S(1)} %get-tuple-element.87), channel_id=1, source_target_pairs={{0,32},{32,0},{64,96},{96,64},{1,33},{33,1},{65,97},{97,65},{2,34}... | collective-permute-start | bytes 208904 | tf_op jit(solution)/shard_map/ppermute | solution.py:428
  134.1 3.6 %collective-permute-start.22 = (f32[18,2,128]{2,1,0:T(2,128)S(1)}, f32[18,2,128]{2,1,0:T(2,128)S(1)}, u32[]{:S(2)}, u32[]{:S(2)}) collective-permute-start(f32[18,2,128]{2,1,0:T(2,128)S(1)} %get-tuple-element.89), channel_id=1, source_target_pairs={{0,1},{1,0},{2,3},{3,2},{4,5},{5,4},{6,7},{7,6},{8,9},{9,8},{10,11... | collective-permute-start | bytes 55304 | tf_op jit(solution)/shard_map/ppermute | solution.py:428
  137.8 5.7 %collective-permute-start.23 = (f32[18,2,128]{2,1,0:T(2,128)S(1)}, f32[18,2,128]{2,1,0:T(2,128)S(1)}, u32[]{:S(2)}, u32[]{:S(2)}) collective-permute-start(f32[18,2,128]{2,1,0:T(2,128)S(1)} %get-tuple-element.90), channel_id=1, source_target_pairs={{0,31},{1,2},{2,1},{3,4},{4,3},{5,6},{6,5},{7,8},{8,7},{9,10},{10,... | collective-permute-start | bytes 55304 | tf_op jit(solution)/shard_map/ppermute | solution.py:428
  143.5 9.4 %collective-permute-start.21 = (f32[17,8,128]{2,1,0:T(8,128)S(1)}, f32[17,8,128]{2,1,0:T(8,128)S(1)}, u32[]{:S(2)}, u32[]{:S(2)}) collective-permute-start(f32[17,8,128]{2,1,0:T(8,128)S(1)} %get-tuple-element.88), channel_id=1, source_target_pairs={{0,96},{32,64},{64,32},{96,0},{1,97},{33,65},{65,33},{97,1},{2,98}... | collective-permute-start | bytes 208904 | tf_op jit(solution)/shard_map/ppermute | solution.py:428
  152.9 1.9 %collective-permute-start.24 = (f32[128]{0:T(128)S(1)}, f32[128]{0:T(128)S(1)}, u32[]{:S(2)}, u32[]{:S(2)}) collective-permute-start(f32[128]{0:T(128)S(1)} %fusion), channel_id=1, source_target_pairs={{0,512},{128,640},{256,768},{384,896},{512,0},{640,128},{768,256},... | collective-permute-start | bytes 1544 | tf_op jit(solution)/shard_map/ppermute | solution.py:456
  154.9 6.1 %collective-permute-done.21.yb_ref = f32[17,8,128]{2,1,0:T(8,128)S(1)} collective-permute-done((f32[17,8,128]{2,1,0:T(8,128)S(1)}, f32[17,8,128]{2,1,0:T(8,128)S(1)}, u32[]{:S(2)}, u32[]{:S(2)}) %collective-permute-start.21) | collective-permute-done | bytes 69664 | tf_op jit(solution)/shard_map/ppermute | solution.py:428
  161.0 3.5 %shard_map.36 = f32[4,18,4,128]{3,2,1,0:T(4,128)} custom-call(s32[3]{0:T(128)S(1)} %pad_add_fusion.where_ref, f32[18,16,128]{2,1,0:T(8,128)S(1)} %get-tuple-element.77.s_ref, f32[18,8,128]{2,1,0:T(8,128)S(1)} %get-tuple-element.83.xp_ref, f32[18,8,128]{2,1,0:T(8,128)S(1)} %get-tuple-element.84.xm_ref, f32[18,16,128]{2,1,0:T(8,128)S(1)} %get-tuple-element.85.tp_ref, ...), custom_call_target="tpu_custom_call" | custom-call | tf_op jit(solution)/shard_map/pallas_call | solution.py:392
  164.6 0.6 slice_reduce_fusion
  (16 shorter events, 0.1 us)
Async XLA Ops:
  0.7 0.9 copy-start
  2.2 29.6 %collective-permute-start.3 = (f32[12,16,128]{2,1,0:T(8,128)S(1)}, f32[12,16,128]{2,1,0:T(8,128)S(1)}, u32[]{:S(2)}, u32[]{:S(2)}) collective-permute-start(f32[12,16,128]{2,1,0:T(8,128)S(1)} %get-tuple-element.51), channel_id=1, source_target_pairs={{0,31},{1,2},{2,1},{3,4},{4,3},{5,6},{6,5},{7,8},{8,7},{9,10},{10,... | collective-permute-start | bytes 294920 | tf_op jit(solution)/shard_map/ppermute | solution.py:428
  10.4 21.5 %collective-permute-start.2 = (f32[12,16,128]{2,1,0:T(8,128)S(1)}, f32[12,16,128]{2,1,0:T(8,128)S(1)}, u32[]{:S(2)}, u32[]{:S(2)}) collective-permute-start(f32[12,16,128]{2,1,0:T(8,128)S(1)} %get-tuple-element.51), channel_id=1, source_target_pairs={{0,1},{1,0},{2,3},{3,2},{4,5},{5,4},{6,7},{7,6},{8,9},{9,8},{10,11... | collective-permute-start | bytes 294920 | tf_op jit(solution)/shard_map/ppermute | solution.py:428
  12.3 18.0 %collective-permute-start = (f32[13,8,128]{2,1,0:T(8,128)S(1)}, f32[13,8,128]{2,1,0:T(8,128)S(1)}, u32[]{:S(2)}, u32[]{:S(2)}) collective-permute-start(f32[13,8,128]{2,1,0:T(8,128)S(1)} %get-tuple-element.49), channel_id=1, source_target_pairs={{0,128},{128,0},{256,384},{384,256},{512,640},{640,512},{768,896},... | collective-permute-start | bytes 159752 | tf_op jit(solution)/shard_map/ppermute | solution.py:428
  16.3 15.5 %collective-permute-start.1 = (f32[13,8,128]{2,1,0:T(8,128)S(1)}, f32[13,8,128]{2,1,0:T(8,128)S(1)}, u32[]{:S(2)}, u32[]{:S(2)}) collective-permute-start(f32[13,8,128]{2,1,0:T(8,128)S(1)} %get-tuple-element.50), channel_id=1, source_target_pairs={{0,896},{128,256},{256,128},{384,512},{512,384},{640,768},{768,640... | collective-permute-start | bytes 159752 | tf_op jit(solution)/shard_map/ppermute | solution.py:428
  33.2 29.8 %collective-permute-start.4 = (f32[18,8,128]{2,1,0:T(8,128)S(1)}, f32[18,8,128]{2,1,0:T(8,128)S(1)}, u32[]{:S(2)}, u32[]{:S(2)}) collective-permute-start(f32[18,8,128]{2,1,0:T(8,128)S(1)} %get-tuple-element.56), channel_id=1, source_target_pairs={{0,32},{32,0},{64,96},{96,64},{1,33},{33,1},{65,97},{97,65},{2,34}... | collective-permute-start | bytes 221192 | tf_op jit(solution)/shard_map/ppermute | solution.py:428
  38.0 25.0 %collective-permute-start.5 = (f32[18,8,128]{2,1,0:T(8,128)S(1)}, f32[18,8,128]{2,1,0:T(8,128)S(1)}, u32[]{:S(2)}, u32[]{:S(2)}) collective-permute-start(f32[18,8,128]{2,1,0:T(8,128)S(1)} %get-tuple-element.57), channel_id=1, source_target_pairs={{0,96},{32,64},{64,32},{96,0},{1,97},{33,65},{65,33},{97,1},{2,98}... | collective-permute-start | bytes 221192 | tf_op jit(solution)/shard_map/ppermute | solution.py:428
  51.5 6.3 %collective-permute-start.6 = (f32[18,2,128]{2,1,0:T(2,128)S(1)}, f32[18,2,128]{2,1,0:T(2,128)S(1)}, u32[]{:S(2)}, u32[]{:S(2)}) collective-permute-start(f32[18,2,128]{2,1,0:T(2,128)S(1)} %get-tuple-element.58), channel_id=1, source_target_pairs={{0,1},{1,0},{2,3},{3,2},{4,5},{5,4},{6,7},{7,6},{8,9},{9,8},{10,11... | collective-permute-start | bytes 55304 | tf_op jit(solution)/shard_map/ppermute | solution.py:428
  55.1 7.8 %collective-permute-start.7 = (f32[18,2,128]{2,1,0:T(2,128)S(1)}, f32[18,2,128]{2,1,0:T(2,128)S(1)}, u32[]{:S(2)}, u32[]{:S(2)}) collective-permute-start(f32[18,2,128]{2,1,0:T(2,128)S(1)} %get-tuple-element.59), channel_id=1, source_target_pairs={{0,31},{1,2},{2,1},{3,4},{4,3},{5,6},{6,5},{7,8},{8,7},{9,10},{10,... | collective-permute-start | bytes 55304 | tf_op jit(solution)/shard_map/ppermute | solution.py:428
  65.8 17.8 %collective-permute-start.11 = (f32[8,16,128]{2,1,0:T(8,128)S(1)}, f32[8,16,128]{2,1,0:T(8,128)S(1)}, u32[]{:S(2)}, u32[]{:S(2)}) collective-permute-start(f32[8,16,128]{2,1,0:T(8,128)S(1)} %get-tuple-element.64), channel_id=1, source_target_pairs={{0,31},{1,2},{2,1},{3,4},{4,3},{5,6},{6,5},{7,8},{8,7},{9,10},{10,... | collective-permute-start | bytes 196616 | tf_op jit(solution)/shard_map/ppermute | solution.py:428
  68.4 15.2 %collective-permute-start.10 = (f32[8,16,128]{2,1,0:T(8,128)S(1)}, f32[8,16,128]{2,1,0:T(8,128)S(1)}, u32[]{:S(2)}, u32[]{:S(2)}) collective-permute-start(f32[8,16,128]{2,1,0:T(8,128)S(1)} %get-tuple-element.64), channel_id=1, source_target_pairs={{0,1},{1,0},{2,3},{3,2},{4,5},{5,4},{6,7},{7,6},{8,9},{9,8},{10,11... | collective-permute-start | bytes 196616 | tf_op jit(solution)/shard_map/ppermute | solution.py:428
  70.4 9.6 %collective-permute-start.8 = (f32[9,8,128]{2,1,0:T(8,128)S(1)}, f32[9,8,128]{2,1,0:T(8,128)S(1)}, u32[]{:S(2)}, u32[]{:S(2)}) collective-permute-start(f32[9,8,128]{2,1,0:T(8,128)S(1)} %get-tuple-element.62), channel_id=1, source_target_pairs={{0,128},{128,0},{256,384},{384,256},{512,640},{640,512},{768,896},... | collective-permute-start | bytes 110600 | tf_op jit(solution)/shard_map/ppermute | solution.py:428
  72.3 11.3 %collective-permute-start.9 = (f32[9,8,128]{2,1,0:T(8,128)S(1)}, f32[9,8,128]{2,1,0:T(8,128)S(1)}, u32[]{:S(2)}, u32[]{:S(2)}) collective-permute-start(f32[9,8,128]{2,1,0:T(8,128)S(1)} %get-tuple-element.63), channel_id=1, source_target_pairs={{0,896},{128,256},{256,128},{384,512},{512,384},{640,768},{768,640... | collective-permute-start | bytes 110600 | tf_op jit(solution)/shard_map/ppermute | solution.py:428
  85.0 21.4 %collective-permute-start.12 = (f32[17,8,128]{2,1,0:T(8,128)S(1)}, f32[17,8,128]{2,1,0:T(8,128)S(1)}, u32[]{:S(2)}, u32[]{:S(2)}) collective-permute-start(f32[17,8,128]{2,1,0:T(8,128)S(1)} %get-tuple-element.70), channel_id=1, source_target_pairs={{0,32},{32,0},{64,96},{96,64},{1,33},{33,1},{65,97},{97,65},{2,34}... | collective-permute-start | bytes 208904 | tf_op jit(solution)/shard_map/ppermute | solution.py:428
  90.0 16.5 %collective-permute-start.13 = (f32[17,8,128]{2,1,0:T(8,128)S(1)}, f32[17,8,128]{2,1,0:T(8,128)S(1)}, u32[]{:S(2)}, u32[]{:S(2)}) collective-permute-start(f32[17,8,128]{2,1,0:T(8,128)S(1)} %get-tuple-element.71), channel_id=1, source_target_pairs={{0,96},{32,64},{64,32},{96,0},{1,97},{33,65},{65,33},{97,1},{2,98}... | collective-permute-start | bytes 208904 | tf_op jit(solution)/shard_map/ppermute | solution.py:428
  95.0 7.0 %collective-permute-start.14 = (f32[18,2,128]{2,1,0:T(2,128)S(1)}, f32[18,2,128]{2,1,0:T(2,128)S(1)}, u32[]{:S(2)}, u32[]{:S(2)}) collective-permute-start(f32[18,2,128]{2,1,0:T(2,128)S(1)} %get-tuple-element.72), channel_id=1, source_target_pairs={{0,1},{1,0},{2,3},{3,2},{4,5},{5,4},{6,7},{7,6},{8,9},{9,8},{10,11... | collective-permute-start | bytes 55304 | tf_op jit(solution)/shard_map/ppermute | solution.py:428
  98.6 7.8 %collective-permute-start.15 = (f32[18,2,128]{2,1,0:T(2,128)S(1)}, f32[18,2,128]{2,1,0:T(2,128)S(1)}, u32[]{:S(2)}, u32[]{:S(2)}) collective-permute-start(f32[18,2,128]{2,1,0:T(2,128)S(1)} %get-tuple-element.73), channel_id=1, source_target_pairs={{0,31},{1,2},{2,1},{3,4},{4,3},{5,6},{6,5},{7,8},{8,7},{9,10},{10,... | collective-permute-start | bytes 55304 | tf_op jit(solution)/shard_map/ppermute | solution.py:428
  109.4 19.5 %collective-permute-start.19 = (f32[8,16,128]{2,1,0:T(8,128)S(1)}, f32[8,16,128]{2,1,0:T(8,128)S(1)}, u32[]{:S(2)}, u32[]{:S(2)}) collective-permute-start(f32[8,16,128]{2,1,0:T(8,128)S(1)} %get-tuple-element.81), channel_id=1, source_target_pairs={{0,31},{1,2},{2,1},{3,4},{4,3},{5,6},{6,5},{7,8},{8,7},{9,10},{10,... | collective-permute-start | bytes 196616 | tf_op jit(solution)/shard_map/ppermute | solution.py:428
  113.7 15.2 %collective-permute-start.18 = (f32[8,16,128]{2,1,0:T(8,128)S(1)}, f32[8,16,128]{2,1,0:T(8,128)S(1)}, u32[]{:S(2)}, u32[]{:S(2)}) collective-permute-start(f32[8,16,128]{2,1,0:T(8,128)S(1)} %get-tuple-element.81), channel_id=1, source_target_pairs={{0,1},{1,0},{2,3},{3,2},{4,5},{5,4},{6,7},{7,6},{8,9},{9,8},{10,11... | collective-permute-start | bytes 196616 | tf_op jit(solution)/shard_map/ppermute | solution.py:428
  115.7 9.6 %collective-permute-start.16 = (f32[9,8,128]{2,1,0:T(8,128)S(1)}, f32[9,8,128]{2,1,0:T(8,128)S(1)}, u32[]{:S(2)}, u32[]{:S(2)}) collective-permute-start(f32[9,8,128]{2,1,0:T(8,128)S(1)} %get-tuple-element.79), channel_id=1, source_target_pairs={{0,128},{128,0},{256,384},{384,256},{512,640},{640,512},{768,896},... | collective-permute-start | bytes 110600 | tf_op jit(solution)/shard_map/ppermute | solution.py:428
  117.6 11.3 %collective-permute-start.17 = (f32[9,8,128]{2,1,0:T(8,128)S(1)}, f32[9,8,128]{2,1,0:T(8,128)S(1)}, u32[]{:S(2)}, u32[]{:S(2)}) collective-permute-start(f32[9,8,128]{2,1,0:T(8,128)S(1)} %get-tuple-element.80), channel_id=1, source_target_pairs={{0,896},{128,256},{256,128},{384,512},{512,384},{640,768},{768,640... | collective-permute-start | bytes 110600 | tf_op jit(solution)/shard_map/ppermute | solution.py:428
  130.3 22.6 %collective-permute-start.20 = (f32[17,8,128]{2,1,0:T(8,128)S(1)}, f32[17,8,128]{2,1,0:T(8,128)S(1)}, u32[]{:S(2)}, u32[]{:S(2)}) collective-permute-start(f32[17,8,128]{2,1,0:T(8,128)S(1)} %get-tuple-element.87), channel_id=1, source_target_pairs={{0,32},{32,0},{64,96},{96,64},{1,33},{33,1},{65,97},{97,65},{2,34}... | collective-permute-start | bytes 208904 | tf_op jit(solution)/shard_map/ppermute | solution.py:428
  134.1 20.7 %collective-permute-start.22 = (f32[18,2,128]{2,1,0:T(2,128)S(1)}, f32[18,2,128]{2,1,0:T(2,128)S(1)}, u32[]{:S(2)}, u32[]{:S(2)}) collective-permute-start(f32[18,2,128]{2,1,0:T(2,128)S(1)} %get-tuple-element.89), channel_id=1, source_target_pairs={{0,1},{1,0},{2,3},{3,2},{4,5},{5,4},{6,7},{7,6},{8,9},{9,8},{10,11... | collective-permute-start | bytes 55304 | tf_op jit(solution)/shard_map/ppermute | solution.py:428
  137.8 17.1 %collective-permute-start.23 = (f32[18,2,128]{2,1,0:T(2,128)S(1)}, f32[18,2,128]{2,1,0:T(2,128)S(1)}, u32[]{:S(2)}, u32[]{:S(2)}) collective-permute-start(f32[18,2,128]{2,1,0:T(2,128)S(1)} %get-tuple-element.90), channel_id=1, source_target_pairs={{0,31},{1,2},{2,1},{3,4},{4,3},{5,6},{6,5},{7,8},{8,7},{9,10},{10,... | collective-permute-start | bytes 55304 | tf_op jit(solution)/shard_map/ppermute | solution.py:428
  143.5 17.5 %collective-permute-start.21 = (f32[17,8,128]{2,1,0:T(8,128)S(1)}, f32[17,8,128]{2,1,0:T(8,128)S(1)}, u32[]{:S(2)}, u32[]{:S(2)}) collective-permute-start(f32[17,8,128]{2,1,0:T(8,128)S(1)} %get-tuple-element.88), channel_id=1, source_target_pairs={{0,96},{32,64},{64,32},{96,0},{1,97},{33,65},{65,33},{97,1},{2,98}... | collective-permute-start | bytes 208904 | tf_op jit(solution)/shard_map/ppermute | solution.py:428
  152.9 11.6 %collective-permute-start.24 = (f32[128]{0:T(128)S(1)}, f32[128]{0:T(128)S(1)}, u32[]{:S(2)}, u32[]{:S(2)}) collective-permute-start(f32[128]{0:T(128)S(1)} %fusion), channel_id=1, source_target_pairs={{0,512},{128,640},{256,768},{384,896},{512,0},{640,128},{768,256},... | collective-permute-start | bytes 1544 | tf_op jit(solution)/shard_map/ppermute | solution.py:456
